TPU v7x, 32 devices: a whole 2x2x4 slice. The times are simulated.
32 devices in a mesh: groups: 2 (over x), section: 8 (over z, y), head: 2 (over core).
Axes of the slice: x: 2, y: 2, z: 4, core: 2. Of those that a mesh axis runs over, the one named last changes fastest.
Arguments:
- video_tokens: bfloat16 [8192, 1536], P(('groups', 'section', 'head')), parts along dimension 0, may hold values from -6 to 6
- modulation: float32 [6, 1536], P('groups'), parts along dimension 0, may hold values from -3 to 3
- project_weight: bfloat16 [3, 1536, 1536], P(None, None, 'head'), may hold values from -0.15625 to 0.15625
- output_weight: bfloat16 [1536, 1536], P('head'), may hold values from -0.15625 to 0.15625
- norm_gains: float32 [3, 128], replicated, may hold values from 1 to 2
- text_cache: bfloat16 [2, 512, 1536], P(None, 'groups', 'head'), parts along dimension 1, may hold values from -6 to 6
- text_count: int32 [2], P('groups'), parts along dimension 0, may hold values from 1 to 256, as said below
- video_keep: int32 [8192], P('groups'), parts along dimension 0, may hold values 0 or 1
- patch_order: int32 [16], P('groups'), parts along dimension 0, may hold values from 0 to 7, each once
- stale_cache: bfloat16 [2, 8192, 1536], P(None, ('groups', 'section'), 'head'), parts along dimension 1, may hold values from -6 to 6
Outputs:
- updated: bfloat16 [8192, 1536], P(('groups', 'section', 'head')), parts along dimension 0
- fresh_cache: bfloat16 [2, 8192, 1536], P(None, ('groups', 'section'), 'head'), parts along dimension 1
There are 2 independent parts, one for each index of `groups`. A program takes and returns all parts, laid end to end along the dimension named above; an argument that names none is the same for every part. Nothing has to cross between parts.
Inputs may be any that keep to these rules, and one draw needn't show every extreme that they name: The first text_count text tokens are real, the rest are padding. `video_keep`: 1 keeps a video token as a key, 0 marks padding. `patch_order`: each place 0 to 7 is held by exactly one patch.
All inputs are finite; a program needn't handle non-finite values.
Results may differ from a plain program's by a relative error of at most 0.0049.
Values may be sent and summed in bfloat16 or wider, within the bound.
A program may use at most 128 MiB of HBM per device.

v0:
```python
import jax
import jax.numpy as jnp
from jax import lax
from jax.sharding import PartitionSpec as P

epsilon = 1e-06


def from_behind(array, axis, by):
    count = lax.axis_size(axis)
    pairs = [(i, i + by) for i in range(count) if 0 <= i + by < count]
    return lax.ppermute(array, axis, pairs)


def layer_norm(values):
    center = jnp.mean(values, axis=-1, keepdims=True)
    shifted = values - center
    spread = jnp.mean(shifted * shifted, axis=-1, keepdims=True)
    return shifted * lax.rsqrt(spread + epsilon)


def head_norm(inputs, gain_row):
    heads_local = inputs.shape[-1] // gain_row.shape[0]
    per_head = inputs.astype(jnp.float32).reshape(inputs.shape[0], heads_local, gain_row.shape[0])
    scaled = (
        per_head
        * lax.rsqrt(jnp.mean(per_head * per_head, axis=-1, keepdims=True) + epsilon)
        * gain_row
    )
    return scaled.astype(jnp.bfloat16)


def lookup(entries, wanted):
    positions = jnp.arange(entries.shape[0], dtype=jnp.int32)
    return jnp.sum(jnp.where(positions == wanted, entries, 0))


def attend_block(queries, key_rows, values, key_live, score_scale):
    scores = (
        jnp.einsum("qhd,khd->hqk", queries, key_rows, preferred_element_type=jnp.float32)
        * score_scale
    )
    weights = jnp.where(key_live[None, None, :], jnp.exp(scores), 0.0)
    total = jnp.sum(weights, axis=-1)
    numerator = jnp.einsum(
        "hqk,khd->qhd", weights.astype(jnp.bfloat16), values, preferred_element_type=jnp.float32
    )
    return (numerator / jnp.transpose(total)[:, :, None]).astype(jnp.bfloat16)


def on_device(
    video_tokens,
    modulation,
    project_weight,
    output_weight,
    norm_gains,
    text_cache,
    text_count,
    video_keep,
    patch_order,
    stale_cache,
):
    section_count = lax.axis_size("section")
    section_place = lax.axis_index("section")
    head_size = norm_gains.shape[1]
    local_width = project_weight.shape[2]
    local_heads = local_width // head_size
    patch_size = stale_cache.shape[1]
    text_rows = text_cache.shape[1]
    hidden = video_tokens.astype(jnp.float32)
    normed = (layer_norm(hidden) * (1.0 + modulation[1]) + modulation[0]).astype(jnp.bfloat16)
    segment = lax.all_gather(normed, "head", axis=0, tiled=True)
    joined = jnp.einsum("rd,cdh->rch", segment, project_weight, preferred_element_type=jnp.float32)
    projected = joined.reshape(segment.shape[0], 3 * local_width)
    key_raw = projected[:, local_width : 2 * local_width].astype(jnp.bfloat16)
    value_raw = projected[:, 2 * local_width :].astype(jnp.bfloat16)
    fresh_cache = jnp.stack([key_raw, value_raw])
    own_slot = lookup(patch_order, section_place)
    left_place = jnp.maximum(section_place - 1, 0)
    right_place = jnp.minimum(section_place + 1, section_count - 1)
    left_slot = lookup(patch_order, left_place)
    right_slot = lookup(patch_order, right_place)
    to_right = jnp.where(own_slot < right_slot, fresh_cache, stale_cache)
    to_left = jnp.where(own_slot < left_slot, fresh_cache, stale_cache)
    left_cache = from_behind(to_right, "section", 1)
    right_cache = from_behind(to_left, "section", -1)
    keep_left = lax.dynamic_slice_in_dim(video_keep, left_place * patch_size, patch_size) > 0
    keep_own = lax.dynamic_slice_in_dim(video_keep, section_place * patch_size, patch_size) > 0
    keep_right = lax.dynamic_slice_in_dim(video_keep, right_place * patch_size, patch_size) > 0
    text_live = jnp.arange(text_rows, dtype=jnp.int32) < text_count[0]
    key_live = jnp.concatenate(
        [
            keep_left & (section_place > 0),
            keep_own,
            keep_right & (section_place < section_count - 1),
            text_live,
        ]
    )
    video_keys = head_norm(
        jnp.concatenate([left_cache[0], key_raw, right_cache[0]], axis=0), norm_gains[1]
    )
    text_keys = head_norm(text_cache[0], norm_gains[2])
    all_keys = jnp.concatenate([video_keys, text_keys], axis=0)
    values = jnp.concatenate(
        [left_cache[1], value_raw, right_cache[1], text_cache[1]], axis=0
    ).reshape(-1, local_heads, head_size)
    queries = head_norm(projected[:, :local_width], norm_gains[0])
    block_rows = min(patch_size, 512)
    score_scale = head_size ** (-0.5)

    def attend(query_block):
        return attend_block(query_block, all_keys, values, key_live, score_scale)

    attended = lax.map(
        attend, queries.reshape(patch_size // block_rows, block_rows, local_heads, head_size)
    ).reshape(patch_size, local_width)
    mixed_rows = lax.psum_scatter(
        jnp.dot(attended, output_weight, preferred_element_type=jnp.float32).astype(jnp.bfloat16),
        "head",
        scatter_dimension=0,
        tiled=True,
    ).astype(jnp.float32)
    updated = (hidden + modulation[2] * mixed_rows).astype(jnp.bfloat16)
    return (updated, fresh_cache)


def solution(mesh):
    placed = (
        P(("groups", "section", "head"), None),
        P("groups", None),
        P(None, None, "head"),
        P("head", None),
        P(),
        P(None, "groups", "head"),
        P("groups"),
        P("groups"),
        P("groups"),
        P(None, ("groups", "section"), "head"),
    )
    return jax.shard_map(
        on_device,
        mesh=mesh,
        in_specs=placed,
        out_specs=(P(("groups", "section", "head"), None), P(None, ("groups", "section"), "head")),
        check_vma=False,
    )
```

profile of v0, /device:TPU:0, one launch (start us, length us, event | category | flops | bytes accessed | tf_op | source)
XLA Modules:
  0.0 167.2 jit_solution(6660057801251343888)
XLA Ops:
  8.7 1.5 fusion.23
  11.1 2.4 %fusion.26 = bf16[256,1536]{1,0:T(8,128)(2,1)} fusion(bf16[256,1536]{1,0:T(8,128)(2,1)} %param.10, f32[1536]{0:T(1024)S(1)} %get-tuple-element.17, f32[1536]{0:T(1024)S(1)} %get-tuple-element.24, f32[256]{0:T(256)S(1)} %add_rsqrt_fusion.3, f32[256]{0:T(256)S(1)} %broadcast_multiply_fusion), kind=kLoop, calls=%fused_computation.33 | loop fusion | flops 2359296 | bytes 1587200 | tf_op jit(solution)/shard_map/convert_element_type | solution.py:71
  17.5 2.6 %copy.18 = bf16[2,512,768]{1,2,0:T(8,128)(2,1)} copy(bf16[2,512,768]{2,1,0:T(8,128)(2,1)} %param.19) | data formatting | bytes 3145728 | tf_op args[9]
  21.0 5.2 %all-gather.2.cloned.1.call-done = bf16[512,1536]{1,0:T(8,128)(2,1)} async-done(((bf16[256,1536]{1,0:T(8,128)(2,1)}), bf16[512,1536]{1,0:T(8,128)(2,1)}) %all-gather.2.cloned.1.call-update) | async-done | bytes 1572880 | tf_op jit(solution)/shard_map/all_gather | solution.py:72
  26.2 6.6 %fusion.29 = f32[512,3,768]{0,2,1:T(8,128)S(1)} fusion(bf16[3,1536,768]{2,1,0:T(8,128)(2,1)} %param.12, bf16[512,1536]{1,0:T(8,128)(2,1)} %all-gather.2.cloned.1.call-done), kind=kOutput, calls=%fused_computation.38 | convolution fusion | flops 3623878656 | bytes 13369344 | tf_op jit(solution)/shard_map/rd,cdh->rch/dot_general | solution.py:73
  33.1 1.8 %copy-done.2 = f32[512,3,768]{0,2,1:T(8,128)} copy-done((f32[512,3,768]{0,2,1:T(8,128)}, f32[512,3,768]{0,2,1:T(8,128)S(1)}, u32[]{:S(2)}) %copy-start.2) | copy-done | bytes 4718616
  36.8 2.5 %broadcast_select_fusion.1 = (bf16[2,512,768]{1,2,0:T(8,128)(2,1)}, bf16[2,512,768]{1,2,0:T(8,128)(2,1)}, bf16[2,512,768]{1,2,0:T(8,128)(2,1)}) fusion(bf16[2,512,768]{1,2,0:T(8,128)(2,1)S(1)} %copy-done.6, pred[]{:T(512)S(6)} %lt.25, bf16[1,512,768]{1,2,0:T(8,128)(2,1)S(1)} %get-tuple-element.32, bf16[1,512,768]{1,2,0:T(8,128)(2,1)S(1)} %get-tuple-element.31, ...), kind=kLoop, calls=%fused_computation.43 | loop fusion | flops 2359296 | bytes 7864322 | tf_op jit(solution)/shard_map/jit(_where)/select_n | solution.py:83
  39.3 4.8 %collective-permute-start = (bf16[2,512,768]{1,2,0:T(8,128)(2,1)}, bf16[2,512,768]{1,2,0:T(8,128)(2,1)}, u32[]{:S(2)}, u32[]{:S(2)}) collective-permute-start(bf16[2,512,768]{1,2,0:T(8,128)(2,1)} %get-tuple-element.28), channel_id=1, source_target_pairs={{0,2},{2,4},{4,6},{6,8},{8,10},{10,12},{12,14},{1,3},{3,5},{5,7},{... | collective-permute-start | bytes 4718600 | tf_op jit(solution)/shard_map/ppermute | solution.py:12
  49.4 2.7 %slice.66 = f32[512,768]{0,1:T(8,128)} slice(f32[512,2304]{0,1:T(8,128)} %bitcast.36), slice={[0:512], [0:768]} | slice | bytes 3145728 | tf_op jit(solution)/shard_map/slice | solution.py:107
  52.1 1.5 copy.22
  53.6 1.6 multiply_reduce_fusion
  55.2 55.9 %collective-permute-done = bf16[2,512,768]{1,2,0:T(8,128)(2,1)} collective-permute-done((bf16[2,512,768]{1,2,0:T(8,128)(2,1)}, bf16[2,512,768]{1,2,0:T(8,128)(2,1)}, u32[]{:S(2)}, u32[]{:S(2)}) %collective-permute-start) | collective-permute-done | bytes 1572896 | tf_op jit(solution)/shard_map/ppermute | solution.py:12
  111.1 2.6 %fusion.47 = (bf16[1,512,768]{1,2,0:T(8,128)(2,1)}, bf16[1,512,768]{1,2,0:T(8,128)(2,1)}) fusion(bf16[2,512,768]{1,2,0:T(8,128)(2,1)} %collective-permute-done), kind=kLoop, calls=%fused_computation.80 | loop fusion | bytes 3145728 | tf_op jit(solution)/shard_map/slice | solution.py:105
  113.7 2.3 %copy.21 = bf16[512,6,128]{2,0,1:T(8,128)(2,1)} copy(bf16[512,6,128]{0,2,1:T(8,128)(2,1)} %bitcast.42) | data formatting | bytes 1572864 | tf_op jit(solution)/shard_map/concatenate | solution.py:100
  116.0 2.6 %fusion.48 = (bf16[1,512,768]{1,2,0:T(8,128)(2,1)}, bf16[1,512,768]{1,2,0:T(8,128)(2,1)}) fusion(bf16[2,512,768]{1,2,0:T(8,128)(2,1)} %collective-permute-done.1), kind=kLoop, calls=%fused_computation.81 | loop fusion | bytes 3145728 | tf_op jit(solution)/shard_map/slice | solution.py:105
  118.6 2.3 %copy.23 = bf16[512,6,128]{2,0,1:T(8,128)(2,1)} copy(bf16[512,6,128]{0,2,1:T(8,128)(2,1)} %bitcast.43) | data formatting | bytes 1572864 | tf_op jit(solution)/shard_map/concatenate | solution.py:100
  120.9 2.8 %fusion.7 = f32[1536,6]{0,1:T(8,128)S(1)} fusion(bf16[512,6,128]{2,0,1:T(8,128)(2,1)} %copy.23, bf16[512,6,128]{2,0,1:T(8,128)(2,1)S(1)} %copy.22, bf16[512,6,128]{2,0,1:T(8,128)(2,1)} %copy.21), kind=kLoop, calls=%fused_computation.9 | loop fusion | flops 9427968 | bytes 2396160 | tf_op jit(solution)/shard_map/reduce_sum | solution.py:27
  123.8 1.5 fusion.9
  125.4 10.0 %fusion = (f32[6,512]{1,0:T(8,128)S(1)}, f32[6,512,1792]{2,1,0:T(8,128)}) fusion(pred[1792]{0:T(1024)(128)(4,1)S(1)} %pad_add_fusion, bf16[256,6,128]{2,0,1:T(8,128)(2,1)S(1)} %copy-done.12, bf16[1536,6,128]{2,0,1:T(8,128)(2,1)S(1)} %fusion.9, f32[512,6,128]{0,2,1:T(8,128)S(1)} %bitcast.38, f32[128]{0:T(128)S(1)} %copy-done.14, f32[512,6]{0,1:T(8,128)S(1)} %add_rsqrt_fusion.1), kind=kOutput, calls=%fused_computation.1 | convolution fusion | flops 1432482816 | bytes 26372352 | tf_op jit(solution)/shard_map/while/body/eval_jaxpr/qhd,khd->hqk/dot_general | solution.py:40
  135.3 9.9 %fusion.28 = bf16[512,6,128]{0,2,1:T(8,128)(2,1)S(1)} fusion(f32[6,512,1792]{2,1,0:T(8,128)} %get-tuple-element.48, pred[1792]{0:T(1024)(128)(4,1)S(1)} %pad_add_fusion, bf16[256,6,128]{0,2,1:T(8,128)(2,1)S(1)} %bitcast.48, bf16[512,6,128]{0,2,1:T(8,128)(2,1)S(1)} %bitcast.47, bf16[512,6,128]{0,2,1:T(8,128)(2,1)S(1)} %bitcast.44, ...), kind=kOutput, calls=%fused_computation.37 | convolution fusion | flops 1437597696 | bytes 25573120 | tf_op jit(solution)/shard_map/while/body/eval_jaxpr/hqk,khd->qhd/dot_general | solution.py:45
  145.3 2.6 %convolution_convert_fusion = bf16[512,1536]{1,0:T(8,128)(2,1)} fusion(bf16[512,768]{0,1:T(8,128)(2,1)S(1)} %bitcast.45, bf16[768,1536]{1,0:T(8,128)(2,1)S(1)} %copy-done), kind=kOutput, calls=%fused_computation.12 | convolution fusion | flops 1208745984 | bytes 4718592 | tf_op jit(solution)/shard_map/dot_general | solution.py:118
  147.9 2.6 %copy.27 = bf16[2,512,768]{2,1,0:T(8,128)(2,1)} copy(bf16[2,512,768]{1,2,0:T(8,128)(2,1)} %get-tuple-element.34) | data formatting | bytes 3145728
  150.5 7.5 %reduce-scatter.2.cloned.1.call-done = bf16[256,1536]{1,0:T(8,128)(2,1)} async-done(((bf16[512,1536]{1,0:T(8,128)(2,1)}), bf16[256,1536]{1,0:T(8,128)(2,1)}) %reduce-scatter.2.cloned.1.call-update) | async-done | bytes 786448 | tf_op jit(solution)/shard_map/reduce_scatter | solution.py:117
  158.1 2.2 %fusion.27 = bf16[256,1536]{1,0:T(8,128)(2,1)} fusion(bf16[256,1536]{1,0:T(8,128)(2,1)S(1)} %copy-done.1, bf16[256,1536]{1,0:T(8,128)(2,1)} %reduce-scatter.2.cloned.1.call-done, f32[1536]{0:T(1024)S(1)} %get-tuple-element.16), kind=kLoop, calls=%fused_computation.34 | loop fusion | flops 1966080 | bytes 2365440 | tf_op jit(solution)/shard_map/convert_element_type | solution.py:123
  (55 shorter events, 11.5 us)
Async XLA Ops:
  7.2 138.1 %copy-start = (bf16[768,1536]{1,0:T(8,128)(2,1)S(1)}, bf16[768,1536]{1,0:T(8,128)(2,1)}, u32[]{:S(2)}) copy-start(bf16[768,1536]{1,0:T(8,128)(2,1)} %param.13) | copy-start | bytes 7077892
  7.2 7.1 %copy-start.13 = (s32[8]{0:T(128)S(1)}, s32[8]{0:T(128)}, u32[]{:S(2)}) copy-start(s32[8]{0:T(128)} %param.18) | copy-start | bytes 100
  7.2 19.0 %all-gather.2.cloned.1.call-start = ((), (), s32[]{:S(2)}) async-start(), calls=%async_computation.1 | async-start | bytes 2359296 | tf_op jit(solution)/shard_map/all_gather | solution.py:72
  13.5 144.5 %reduce-scatter.2.cloned.1.call-start = ((), (), s32[]{:S(2)}) async-start(), calls=%async_computation.2 | async-start | bytes 2359296 | tf_op jit(solution)/shard_map/reduce_scatter | solution.py:117
  32.8 2.1 %copy-start.2 = (f32[512,3,768]{0,2,1:T(8,128)}, f32[512,3,768]{0,2,1:T(8,128)S(1)}, u32[]{:S(2)}) copy-start(f32[512,3,768]{0,2,1:T(8,128)S(1)} %fusion.29) | copy-start | bytes 14155780
  34.9 1.9 %copy-start.6 = (bf16[2,512,768]{1,2,0:T(8,128)(2,1)S(1)}, bf16[2,512,768]{1,2,0:T(8,128)(2,1)}, u32[]{:S(2)}) copy-start(bf16[2,512,768]{1,2,0:T(8,128)(2,1)} %copy.18) | copy-start | bytes 4718596
  36.8 7.4 %copy-start.8 = (bf16[2,256,768]{2,1,0:T(8,128)(2,1)S(1)}, bf16[2,256,768]{2,1,0:T(8,128)(2,1)}, u32[]{:S(2)}) copy-start(bf16[2,256,768]{2,1,0:T(8,128)(2,1)} %param.15) | copy-start | bytes 2359300
  39.3 71.8 %collective-permute-start = (bf16[2,512,768]{1,2,0:T(8,128)(2,1)}, bf16[2,512,768]{1,2,0:T(8,128)(2,1)}, u32[]{:S(2)}, u32[]{:S(2)}) collective-permute-start(bf16[2,512,768]{1,2,0:T(8,128)(2,1)} %get-tuple-element.28), channel_id=1, source_target_pairs={{0,2},{2,4},{4,6},{6,8},{8,10},{10,12},{12,14},{1,3},{3,5},{5,7},{... | collective-permute-start | bytes 4718600 | tf_op jit(solution)/shard_map/ppermute | solution.py:12
  44.2 71.8 %collective-permute-start.1 = (bf16[2,512,768]{1,2,0:T(8,128)(2,1)}, bf16[2,512,768]{1,2,0:T(8,128)(2,1)}, u32[]{:S(2)}, u32[]{:S(2)}) collective-permute-start(bf16[2,512,768]{1,2,0:T(8,128)(2,1)} %get-tuple-element.29), channel_id=1, source_target_pairs={{2,0},{4,2},{6,4},{8,6},{10,8},{12,10},{14,12},{3,1},{5,3},{7,5},{... | collective-permute-start | bytes 4718600 | tf_op jit(solution)/shard_map/ppermute | solution.py:12
  120.9 2.8 %copy-start.3 = (bf16[512,6,128]{2,0,1:T(8,128)(2,1)S(1)}, bf16[512,6,128]{2,0,1:T(8,128)(2,1)}, u32[]{:S(2)}) copy-start(bf16[512,6,128]{2,0,1:T(8,128)(2,1)} %copy.21) | copy-start | bytes 2359300
  120.9 2.8 %copy-start.4 = (bf16[512,6,128]{2,0,1:T(8,128)(2,1)S(1)}, bf16[512,6,128]{2,0,1:T(8,128)(2,1)}, u32[]{:S(2)}) copy-start(bf16[512,6,128]{2,0,1:T(8,128)(2,1)} %copy.23) | copy-start | bytes 2359300
  123.8 1.5 copy-start.5
  123.8 1.5 copy-start.12
  123.8 1.5 copy-start.14
  125.3 10.0 %copy-start.7 = (bf16[512,768]{0,1:T(8,128)(2,1)S(1)}, bf16[512,768]{0,1:T(8,128)(2,1)}, u32[]{:S(2)}) copy-start(bf16[512,768]{0,1:T(8,128)(2,1)} %get-tuple-element.30) | copy-start | bytes 2359300
  125.3 10.0 %copy-start.9 = (bf16[1,512,768]{1,2,0:T(8,128)(2,1)S(1)}, bf16[1,512,768]{1,2,0:T(8,128)(2,1)}, u32[]{:S(2)}) copy-start(bf16[1,512,768]{1,2,0:T(8,128)(2,1)} %get-tuple-element.35) | copy-start | bytes 2359300
  125.3 10.0 %copy-start.10 = (bf16[1,512,768]{1,2,0:T(8,128)(2,1)S(1)}, bf16[1,512,768]{1,2,0:T(8,128)(2,1)}, u32[]{:S(2)}) copy-start(bf16[1,512,768]{1,2,0:T(8,128)(2,1)} %get-tuple-element.37) | copy-start | bytes 2359300
  125.3 10.0 %copy-start.11 = (bf16[1,256,768]{1,2,0:T(8,128)(2,1)S(1)}, bf16[1,256,768]{1,2,0:T(8,128)(2,1)}, u32[]{:S(2)}) copy-start(bf16[1,256,768]{1,2,0:T(8,128)(2,1)} %copy.20) | copy-start | bytes 1179652
  147.8 10.2 %copy-start.1 = (bf16[256,1536]{1,0:T(8,128)(2,1)S(1)}, bf16[256,1536]{1,0:T(8,128)(2,1)}, u32[]{:S(2)}) copy-start(bf16[256,1536]{1,0:T(8,128)(2,1)} %param.10) | copy-start | bytes 2359300
Sparse Core Ops, SparseCore 0:
  13.6 12.5 all-gather.1
  148.0 10.0 reduce-scatter.1
where the time goes:
time: 168 us; the launch traced here: 167 us
  waiting for transfers between devices  68.7 us (41%)
  matrix products  29 us (17%)
  local copies, waits for them, and re-layouts  25.6 us (15%)
  other arithmetic  19.9 us (12%)
  between operations  17.5 us (10%)
  starting transfers between devices  6.37 us (4%)
    ppermute x2, waiting for transfers between devices, from_behind(): return lax.ppermute(array, axis, pairs)  55.9 us
    dot_general x1, matrix products, attend_block(): jnp.einsum('qhd,khd->hqk', queries, key_rows, preferred_element_type=jnp....  9.97 us
    dot_general x1, matrix products, attend_block(): jnp.einsum('hqk,khd->qhd', weights.astype(jnp.bfloat16), values, preferre...  9.91 us
    unnamed x33, local copies, waits for them, and re-layouts  7.73 us
    reduce_scatter x1, waiting for transfers between devices, on_device(): lax.psum_scatter(jnp.dot(attended, output_weight, preferred_element_type=...  7.55 us
    dot_general x1, matrix products, on_device(): jnp.einsum('rd,cdh->rch', segment, project_weight, preferred_element_type...  6.6 us
    ppermute x2, starting transfers between devices, from_behind(): return lax.ppermute(array, axis, pairs)  6.29 us
    concatenate x3, local copies, waits for them, and re-layouts, on_device(): jnp.concatenate([left_cache[0], key_raw, right_cache[0]], axis=0)  6.08 us
  transfers between devices with their start and end apart: 4, of which 3 were waited for; matrix products, arithmetic and copies ran while one was open for 13% of the time, Pallas kernels for 0%

commit v1 on v0

v1 whole, which is shorter than its diff:
```python
import jax
import jax.numpy as jnp
from jax import lax
from jax.experimental import pallas as pl
from jax.experimental.pallas import tpu as pltpu
from jax.sharding import PartitionSpec as P

epsilon = 1e-06
log2_e = 1.4426950408889634
MESH = pl.DeviceIdType.MESH
f32 = jnp.float32
bf16 = jnp.bfloat16


def dot_nt(a, b):
    return lax.dot_general(a, b, (((1,), (1,)), ((), ())), preferred_element_type=f32)


def head_norm(rows, gain):
    return rows * lax.rsqrt(jnp.mean(rows * rows, axis=-1, keepdims=True) + epsilon) * gain


def kernel(
    order_ref,
    count_ref,
    tokens_ref,
    modulation_ref,
    gains_ref,
    keep_ref,
    weight_hbm,
    output_weight_hbm,
    text_hbm,
    stale_hbm,
    updated_ref,
    fresh_hbm,
    weight,
    output_weight,
    text,
    stale,
    normed,
    raw,
    query,
    query_mate,
    query_far,
    keys,
    values,
    text_keys,
    text_values,
    own_sum,
    mate_sum,
    far_out,
    far_total_out,
    far_in,
    far_total_in,
    back_out,
    back_total_out,
    back_in,
    back_total_in,
    attended,
    mixed_out,
    mixed_in,
    load_sem,
    store_sem,
    normed_sem,
    query_sem,
    forward_sem,
    far_sem,
    far_total_sem,
    back_sem,
    back_total_sem,
    mixed_sem,
):
    count = lax.axis_size("section")
    me = lax.axis_index("section")
    core = lax.axis_index("head")
    other_core = 1 - core
    parity = lax.rem(me, 2)
    mate = me + 1 - 2 * parity
    step = 2 - 4 * parity
    ahead = me + step
    behind = me - step
    has_ahead = jnp.logical_and(ahead >= 0, ahead < count)
    has_behind = jnp.logical_and(behind >= 0, behind < count)
    rows = tokens_ref.shape[0]
    head = gains_ref.shape[1]
    width = weight.shape[2]
    heads = width // head
    units = 2 * heads
    patch = 2 * rows

    loads = [
        pltpu.make_async_copy(weight_hbm.at[c], weight.at[c], load_sem.at[c]) for c in range(3)
    ]
    loads.append(pltpu.make_async_copy(stale_hbm, stale, load_sem.at[3]))
    loads.append(pltpu.make_async_copy(text_hbm, text, load_sem.at[4]))
    loads.append(pltpu.make_async_copy(output_weight_hbm, output_weight, load_sem.at[5]))
    for load in loads:
        load.start()

    barrier = pltpu.get_barrier_semaphore()
    pl.semaphore_signal(barrier, inc=1, device_id={"head": other_core}, device_id_type=MESH)
    pl.semaphore_signal(barrier, inc=1, device_id={"section": mate}, device_id_type=MESH)

    @pl.when(has_ahead)
    def _():
        pl.semaphore_signal(barrier, inc=1, device_id={"section": ahead}, device_id_type=MESH)

    @pl.when(has_behind)
    def _():
        pl.semaphore_signal(barrier, inc=1, device_id={"section": behind}, device_id_type=MESH)

    hidden = tokens_ref[...].astype(f32)
    shifted = hidden - jnp.mean(hidden, axis=-1, keepdims=True)
    spread = jnp.mean(shifted * shifted, axis=-1, keepdims=True)
    normed[0] = (
        shifted * lax.rsqrt(spread + epsilon) * (1.0 + modulation_ref[1:2, :])
        + modulation_ref[0:1, :]
    ).astype(bf16)

    pl.semaphore_wait(
        barrier, 2 + has_ahead.astype(jnp.int32) + has_behind.astype(jnp.int32)
    )

    normed_copy = pltpu.make_async_remote_copy(
        src_ref=normed.at[0],
        dst_ref=normed.at[1],
        send_sem=normed_sem.at[0],
        recv_sem=normed_sem.at[1],
        device_id={"head": other_core},
        device_id_type=MESH,
    )
    normed_copy.start()

    def remote(source, target, sems, unit, device):
        return pltpu.make_async_remote_copy(
            src_ref=source.at[unit],
            dst_ref=target.at[unit],
            send_sem=sems.at[0, unit],
            recv_sem=sems.at[1, unit],
            device_id={"section": device},
            device_id_type=MESH,
        )

    def query_copy(unit):
        return remote(query, query_mate, query_sem, unit, mate)

    def forward_copy(unit, device):
        return remote(query_mate, query_far, forward_sem, unit, device)

    def far_copies(unit, device):
        return (
            remote(far_out, far_in, far_sem, unit, device),
            remote(far_total_out, far_total_in, far_total_sem, unit, device),
        )

    def back_copies(unit):
        return (
            remote(back_out, back_in, back_sem, unit, mate),
            remote(back_total_out, back_total_in, back_total_sem, unit, mate),
        )

    factor = head ** (-0.5) * log2_e
    pair = 2 if heads % 2 == 0 else 1
    span = pair * head

    def columns(step_index):
        return pl.ds(pl.multiple_of(step_index * span, span), span)

    def project_queries(half):
        @pl.loop(0, heads // pair)
        def _(c):
            part = jnp.dot(normed[half], weight[0, :, columns(c)], preferred_element_type=f32)
            for j in range(pair):
                unit = half * heads + c * pair + j
                query[unit] = (
                    head_norm(part[:, j * head : (j + 1) * head], gains_ref[0:1, :]) * factor
                ).astype(bf16)
                query_copy(unit).start()

    def project_caches(half):
        place = core if half == 0 else other_core
        here = pl.ds(pl.multiple_of(place * rows, rows), rows)

        @pl.loop(0, heads // pair)
        def _(c):
            for w in range(2):
                part = jnp.dot(
                    normed[half], weight[1 + w, :, columns(c)], preferred_element_type=f32
                )
                raw[w, here, columns(c)] = part.astype(bf16)

    loads[0].wait()
    project_queries(0)
    loads[1].wait()
    loads[2].wait()
    project_caches(0)
    normed_copy.wait_recv()
    project_queries(1)
    project_caches(1)
    fresh_store = pltpu.make_async_copy(raw, fresh_hbm, store_sem)
    fresh_store.start()
    loads[3].wait()
    loads[4].wait()

    keep_row = keep_ref[pl.ds(me, 1), :].astype(f32)
    keep = jnp.transpose(jnp.broadcast_to(keep_row, (head, patch)))
    text_rows = text.shape[1]
    live = (
        lax.broadcasted_iota(jnp.int32, (text_rows, head), 0) < count_ref[0]
    ).astype(f32)

    @pl.loop(0, heads)
    def _(h):
        lanes = pl.ds(pl.multiple_of(h * head, head), head)
        for version, cache in ((0, raw), (1, stale)):
            keys[version, h] = head_norm(
                cache[0, :, lanes].astype(f32), gains_ref[1:2, :]
            ).astype(bf16)
            values[version, h, :, 0:head] = (cache[1, :, lanes].astype(f32) * keep).astype(bf16)
            values[version, h, :, head : 2 * head] = keep.astype(bf16)
        text_keys[h] = head_norm(text[0, :, lanes].astype(f32), gains_ref[2:3, :]).astype(bf16)
        text_values[h, :, 0:head] = (text[1, :, lanes].astype(f32) * live).astype(bf16)
        text_values[h, :, head : 2 * head] = live.astype(bf16)

    own_slot = order_ref[me]
    mate_version = jnp.where(own_slot < order_ref[mate], 0, 1)
    far_patch = jnp.clip(me - 1 + 2 * parity, 0, count - 1)
    far_version = jnp.where(own_slot < order_ref[far_patch], 0, 1)

    def weighted(queries, key_rows, value_rows):
        weights = jnp.exp2(dot_nt(queries, key_rows)).astype(bf16)
        return jnp.dot(weights, value_rows, preferred_element_type=f32)

    def total_rows(summed):
        return jnp.transpose(summed[:, head : 2 * head])[0:8, :]

    def send_back(unit):
        numerator = mate_sum[unit, :, 0:head]
        totals = total_rows(mate_sum[unit])

        @pl.when(has_ahead)
        def _():
            for copy in far_copies(unit, mate):
                copy.wait_recv()
            back_out[unit] = (numerator + far_in[unit].astype(f32)).astype(bf16)
            back_total_out[unit] = totals + far_total_in[unit]

        @pl.when(jnp.logical_not(has_ahead))
        def _():
            back_out[unit] = numerator.astype(bf16)
            back_total_out[unit] = totals

        for copy in back_copies(unit):
            copy.start()

    @pl.loop(0, units + 3)
    def _(i):
        @pl.when(i < units)
        def _():
            h = lax.rem(i, heads)
            own_sum[i] = weighted(query[i], keys[0, h], values[0, h]) + weighted(
                query[i], text_keys[h], text_values[h]
            )
            query_copy(i).wait_recv()

            @pl.when(has_ahead)
            def _():
                forward_copy(i, ahead).start()

            mate_sum[i] = weighted(query_mate[i], keys[mate_version, h], values[mate_version, h])

        @pl.when(jnp.logical_and(has_behind, jnp.logical_and(i >= 1, i < units + 1)))
        def _():
            unit = i - 1
            h = lax.rem(unit, heads)
            forward_copy(unit, mate).wait_recv()
            summed = weighted(query_far[unit], keys[far_version, h], values[far_version, h])
            far_out[unit] = summed[:, 0:head].astype(bf16)
            far_total_out[unit] = total_rows(summed)
            for copy in far_copies(unit, behind):
                copy.start()

        @pl.when(i >= heads + 3)
        def _():
            send_back(i - 3)

    @pl.loop(0, heads)
    def _(i):
        send_back(i)

    def gather_back(half):
        @pl.loop(0, heads)
        def _(h):
            unit = half * heads + h
            for copy in back_copies(unit):
                copy.wait_recv()
            total = jnp.transpose(
                jnp.broadcast_to(back_total_in[unit, 0:1, :], (head, rows))
            )
            mine = own_sum[unit]
            attended[half, :, pl.ds(pl.multiple_of(h * head, head), head)] = (
                (mine[:, 0:head] + back_in[unit].astype(f32))
                / (mine[:, head : 2 * head] + total)
            ).astype(bf16)

    mixed_copy = pltpu.make_async_remote_copy(
        src_ref=mixed_out,
        dst_ref=mixed_in,
        send_sem=mixed_sem.at[0],
        recv_sem=mixed_sem.at[1],
        device_id={"head": other_core},
        device_id_type=MESH,
    )
    full = output_weight.shape[1]
    wide = 512 if full % 512 == 0 else full

    gather_back(1)
    loads[5].wait()

    @pl.loop(0, full // wide)
    def _(c):
        here = pl.ds(pl.multiple_of(c * wide, wide), wide)
        mixed_out[:, here] = jnp.dot(
            attended[1], output_weight[:, here], preferred_element_type=f32
        ).astype(bf16)

    mixed_copy.start()
    gather_back(0)
    mixed_copy.wait_recv()

    @pl.loop(0, full // wide)
    def _(c):
        here = pl.ds(pl.multiple_of(c * wide, wide), wide)
        mixed = jnp.dot(attended[0], output_weight[:, here], preferred_element_type=f32)
        mixed = mixed + mixed_in[:, here].astype(f32)
        updated_ref[:, here] = (
            tokens_ref[:, here].astype(f32) + modulation_ref[2:3, here] * mixed
        ).astype(bf16)

    fresh_store.wait()
    normed_copy.wait_send()
    mixed_copy.wait_send()

    @pl.loop(0, units)
    def _(i):
        query_copy(i).wait_send()
        for copy in back_copies(i):
            copy.wait_send()

        @pl.when(has_ahead)
        def _():
            forward_copy(i, mate).wait_send()

        @pl.when(has_behind)
        def _():
            for copy in far_copies(i, mate):
                copy.wait_send()


def on_device(
    video_tokens,
    modulation,
    project_weight,
    output_weight,
    norm_gains,
    text_cache,
    text_count,
    video_keep,
    patch_order,
    stale_cache,
):
    head = norm_gains.shape[1]
    rows, model = video_tokens.shape
    width = project_weight.shape[2]
    patch = stale_cache.shape[1]
    text_rows = text_cache.shape[1]
    heads = width // head
    units = 2 * heads
    smem = pl.BlockSpec(memory_space=pltpu.SMEM)
    vmem = pl.BlockSpec(memory_space=pltpu.VMEM)
    hbm = pl.BlockSpec(memory_space=pl.ANY)
    unit_rows = pltpu.VMEM((units, rows, head), bf16)
    unit_totals = pltpu.VMEM((units, 8, rows), f32)
    unit_sums = pltpu.VMEM((units, rows, 2 * head), f32)
    unit_sems = pltpu.SemaphoreType.DMA((2, units))
    return pl.pallas_call(
        kernel,
        out_shape=(
            jax.ShapeDtypeStruct(video_tokens.shape, bf16),
            jax.ShapeDtypeStruct(stale_cache.shape, bf16),
        ),
        in_specs=[smem, smem, vmem, vmem, vmem, vmem, hbm, hbm, hbm, hbm],
        out_specs=(vmem, hbm),
        scratch_shapes=[
            pltpu.VMEM(project_weight.shape, bf16),
            pltpu.VMEM(output_weight.shape, bf16),
            pltpu.VMEM(text_cache.shape, bf16),
            pltpu.VMEM(stale_cache.shape, bf16),
            pltpu.VMEM((2, rows, model), bf16),
            pltpu.VMEM(stale_cache.shape, bf16),
            unit_rows,
            unit_rows,
            unit_rows,
            pltpu.VMEM((2, heads, patch, head), bf16),
            pltpu.VMEM((2, heads, patch, 2 * head), bf16),
            pltpu.VMEM((heads, text_rows, head), bf16),
            pltpu.VMEM((heads, text_rows, 2 * head), bf16),
            unit_sums,
            unit_sums,
            unit_rows,
            unit_totals,
            unit_rows,
            unit_totals,
            unit_rows,
            unit_totals,
            unit_rows,
            unit_totals,
            pltpu.VMEM((2, rows, width), bf16),
            pltpu.VMEM((rows, model), bf16),
            pltpu.VMEM((rows, model), bf16),
            pltpu.SemaphoreType.DMA((6,)),
            pltpu.SemaphoreType.DMA,
            pltpu.SemaphoreType.DMA((2,)),
            unit_sems,
            unit_sems,
            unit_sems,
            unit_sems,
            unit_sems,
            unit_sems,
            pltpu.SemaphoreType.DMA((2,)),
        ],
        compiler_params=pltpu.CompilerParams(
            collective_id=0, has_side_effects=True, vmem_limit_bytes=60 * 1024 * 1024
        ),
    )(
        patch_order,
        text_count,
        video_tokens,
        modulation,
        norm_gains,
        video_keep.reshape(-1, patch),
        project_weight,
        output_weight,
        text_cache,
        stale_cache,
    )


def solution(mesh):
    placed = (
        P(("groups", "section", "head"), None),
        P("groups", None),
        P(None, None, "head"),
        P("head", None),
        P(),
        P(None, "groups", "head"),
        P("groups"),
        P("groups"),
        P("groups"),
        P(None, ("groups", "section"), "head"),
    )
    return jax.shard_map(
        on_device,
        mesh=mesh,
        in_specs=placed,
        out_specs=(P(("groups", "section", "head"), None), P(None, ("groups", "section"), "head")),
        check_vma=False,
    )
```

time: 168 us -> 64.9 us (0.39)
  waiting for transfers between devices: 68.7 us -> 0 us
  Pallas kernels: 0 us -> 58.7 us
  matrix products: 29 us -> 0 us
  local copies, waits for them, and re-layouts: 25.6 us -> 4.65 us
  other arithmetic: 19.9 us -> 0 us
  between operations: 17.5 us -> 1.29 us
  starting transfers between devices: 6.37 us -> 0 us
    pallas_call x0 -> x1, Pallas kernels: none -> 58.7 us  [on_device(): pl.pallas_call(kernel, out_shape=(jax.ShapeDtypeStruct(video_tokens.shape...]
    ppermute x2 -> x0, waiting for transfers between devices: 55.9 us -> none  [from_behind(): return lax.ppermute(array, axis, pairs)]
    dot_general x4 -> x0, matrix products: 29 us -> none  [the longest x1 9.97 us: attend_block(): jnp.einsum('qhd,khd->hqk', queries, key_rows, preferred_element_type=jnp....]
    slice x6 -> x0, local copies, waits for them, and re-layouts: 10.3 us -> none  [the longest x1 2.67 us: on_device(): queries = head_norm(projected[:, :local_width], norm_gains[0])]
    reduce_sum x6 -> x0, other arithmetic: 8.12 us -> none  [the longest x3 4.47 us: head_norm(): jnp.mean(per_head * per_head, axis=-1, keepdims=True) + epsilon]
    reduce_scatter x1 -> x0, waiting for transfers between devices: 7.55 us -> none  [on_device(): lax.psum_scatter(jnp.dot(attended, output_weight, preferred_element_type=...]
    convert_element_type x4 -> x0, other arithmetic: 7.12 us -> none  [the longest x2 2.5 us: head_norm(): return scaled.astype(jnp.bfloat16)]
    ppermute x2 -> x0, starting transfers between devices: 6.29 us -> none  [from_behind(): return lax.ppermute(array, axis, pairs)]
  transfers between devices with their start and end apart: 4 -> 0, of which waited for: 3 -> 0; matrix products, arithmetic and copies ran while one was open for 13% -> 0% of each run, Pallas kernels for 0% -> 0%
where the time goes in v1:
time: 64.9 us; the launch traced here: 64.6 us
  Pallas kernels  58.7 us (90%)
  local copies, waits for them, and re-layouts  4.65 us (7%)
  between operations  1.29 us (2%)
    pallas_call x1, Pallas kernels, on_device(): pl.pallas_call(kernel, out_shape=(jax.ShapeDtypeStruct(video_tokens.shape...  58.7 us
    unnamed x4, local copies, waits for them, and re-layouts  3.33 us
    reshape x1, local copies, waits for them, and re-layouts, on_device(): video_keep.reshape(-1, patch)  1.33 us

profile of v1, /device:TPU:0, one launch (start us, length us, event | category | flops | bytes accessed | tf_op | source)
XLA Modules:
  0.0 64.6 jit_solution(7663288220781032600)
XLA Ops:
  1.3 1.3 %reshape.7.keep_ref = s32[8,512]{1,0:T(8,128)} reshape(s32[4096]{0:T(1024)} %param.17) | data formatting | bytes 32768 | tf_op jit(solution)/shard_map/reshape | solution.py:441
  2.6 58.7 %shard_map.113 = (bf16[256,1536]{1,0:T(8,128)(2,1)}, bf16[2,512,768]{2,1,0:T(8,128)(2,1)}) custom-call(s32[8]{0:T(128)} %order_ref.1, s32[1]{0:T(128)S(6)} %copy.14.count_ref, bf16[256,1536]{1,0:T(8,128)(2,1)} %tokens_ref.1, f32[3,1536]{1,0:T(4,128)} %modulation_ref.1, f32[3,128]{1,0:T(4,128)} %gains_ref.1, s32[8,512]{1,0:T(8,128)} %reshape.7.keep_ref, ...), custom_call_target="tpu_custom_call" | custom-call | tf_op jit(solution)/shard_map/pallas_call | solution.py:386
  61.3 0.0 copy-start
  61.3 2.2 %copy.15 = bf16[256,1536]{1,0:T(8,128)(2,1)} copy(bf16[256,1536]{1,0:T(8,128)(2,1)} %get-tuple-element.4) | data formatting | bytes 1572864
  63.5 0.0 copy-done
  63.5 1.1 %copy.16 = bf16[2,512,768]{2,1,0:T(8,128)(2,1)} copy(bf16[2,512,768]{2,1,0:T(8,128)(2,1)S(1)} %copy-done) | data formatting | bytes 3145728
Async XLA Ops:
  61.3 2.2 %copy-start = (bf16[2,512,768]{2,1,0:T(8,128)(2,1)S(1)}, bf16[2,512,768]{2,1,0:T(8,128)(2,1)}, u32[]{:S(2)}) copy-start(bf16[2,512,768]{2,1,0:T(8,128)(2,1)} %get-tuple-element.5) | copy-start | bytes 4718596

commit v2 on v1

--- a/solution.py
+++ b/solution.py
@@ -23,22 +23,25 @@
 def kernel(
     order_ref,
     count_ref,
-    tokens_ref,
-    modulation_ref,
-    gains_ref,
-    keep_ref,
+    tokens_hbm,
+    modulation_hbm,
+    gains_hbm,
+    keep_hbm,
     weight_hbm,
     output_weight_hbm,
     text_hbm,
     stale_hbm,
     updated_ref,
-    fresh_hbm,
+    raw,
+    tokens_ref,
+    modulation_ref,
+    gains_ref,
+    keep_ref,
     weight,
     output_weight,
     text,
     stale,
     normed,
-    raw,
     query,
     query_mate,
     query_far,
@@ -60,7 +63,6 @@
     mixed_out,
     mixed_in,
     load_sem,
-    store_sem,
     normed_sem,
     query_sem,
     forward_sem,
@@ -81,7 +83,7 @@
     behind = me - step
     has_ahead = jnp.logical_and(ahead >= 0, ahead < count)
     has_behind = jnp.logical_and(behind >= 0, behind < count)
-    rows = tokens_ref.shape[0]
+    rows = tokens_hbm.shape[0]
     head = gains_ref.shape[1]
     width = weight.shape[2]
     heads = width // head
@@ -94,8 +96,20 @@
     loads.append(pltpu.make_async_copy(stale_hbm, stale, load_sem.at[3]))
     loads.append(pltpu.make_async_copy(text_hbm, text, load_sem.at[4]))
     loads.append(pltpu.make_async_copy(output_weight_hbm, output_weight, load_sem.at[5]))
-    for load in loads:
+    small = [
+        pltpu.make_async_copy(source, target, load_sem.at[6 + place])
+        for place, (source, target) in enumerate(
+            (
+                (tokens_hbm, tokens_ref),
+                (modulation_hbm, modulation_ref),
+                (gains_hbm, gains_ref),
+                (keep_hbm, keep_ref),
+            )
+        )
+    ]
+    for load in small:
         load.start()
+    loads[0].start()
 
     barrier = pltpu.get_barrier_semaphore()
     pl.semaphore_signal(barrier, inc=1, device_id={"head": other_core}, device_id_type=MESH)
@@ -109,6 +123,8 @@
     def _():
         pl.semaphore_signal(barrier, inc=1, device_id={"section": behind}, device_id_type=MESH)
 
+    for load in small:
+        load.wait()
     hidden = tokens_ref[...].astype(f32)
     shifted = hidden - jnp.mean(hidden, axis=-1, keepdims=True)
     spread = jnp.mean(shifted * shifted, axis=-1, keepdims=True)
@@ -177,33 +193,50 @@
                 ).astype(bf16)
                 query_copy(unit).start()
 
-    def project_caches(half):
-        place = core if half == 0 else other_core
-        here = pl.ds(pl.multiple_of(place * rows, rows), rows)
-
-        @pl.loop(0, heads // pair)
-        def _(c):
-            for w in range(2):
-                part = jnp.dot(
-                    normed[half], weight[1 + w, :, columns(c)], preferred_element_type=f32
-                )
-                raw[w, here, columns(c)] = part.astype(bf16)
-
+    early = min(3, heads)
+
+    def forward(unit):
+        query_copy(unit).wait_recv()
+
+        @pl.when(has_ahead)
+        def _():
+            forward_copy(unit, ahead).start()
+
+    for load in loads[1:]:
+        load.start()
     loads[0].wait()
     project_queries(0)
+    normed_copy.wait_recv()
+    project_queries(1)
     loads[1].wait()
     loads[2].wait()
-    project_caches(0)
-    normed_copy.wait_recv()
-    project_queries(1)
-    project_caches(1)
-    fresh_store = pltpu.make_async_copy(raw, fresh_hbm, store_sem)
-    fresh_store.start()
+    own_rows = pl.ds(pl.multiple_of(core * rows, rows), rows)
+    other_rows = pl.ds(pl.multiple_of(other_core * rows, rows), rows)
+
+    @pl.loop(0, heads // pair)
+    def _(c):
+        for w in range(2):
+            part = jnp.dot(
+                normed[...].reshape(patch, normed.shape[2]),
+                weight[1 + w, :, columns(c)],
+                preferred_element_type=f32,
+            ).astype(bf16)
+            raw[w, own_rows, columns(c)] = part[0:rows]
+            raw[w, other_rows, columns(c)] = part[rows:patch]
+
+        @pl.when(c < early)
+        def _():
+            forward(c)
+
+    @pl.loop(min(early, heads // pair), early)
+    def _(i):
+        forward(i)
+
     loads[3].wait()
     loads[4].wait()
 
-    keep_row = keep_ref[pl.ds(me, 1), :].astype(f32)
-    keep = jnp.transpose(jnp.broadcast_to(keep_row, (head, patch)))
+    keep_row = keep_ref[pl.ds(pl.multiple_of(me * patch, patch), patch)].astype(f32)
+    keep = jnp.transpose(jnp.broadcast_to(keep_row[None, :], (head, patch)))
     text_rows = text.shape[1]
     live = (
         lax.broadcasted_iota(jnp.int32, (text_rows, head), 0) < count_ref[0]
@@ -232,7 +265,7 @@
         return jnp.dot(weights, value_rows, preferred_element_type=f32)
 
     def total_rows(summed):
-        return jnp.transpose(summed[:, head : 2 * head])[0:8, :]
+        return jnp.transpose(summed[:, head : 2 * head])[0:1, :]
 
     def send_back(unit):
         numerator = mate_sum[unit, :, 0:head]
@@ -253,38 +286,45 @@
         for copy in back_copies(unit):
             copy.start()
 
-    @pl.loop(0, units + 3)
+    ahead_backs = min(2, heads)
+
+    @pl.loop(early, units + 2 * early)
     def _(i):
         @pl.when(i < units)
         def _():
-            h = lax.rem(i, heads)
-            own_sum[i] = weighted(query[i], keys[0, h], values[0, h]) + weighted(
-                query[i], text_keys[h], text_values[h]
+            forward(i)
+
+        unit = i - early
+
+        @pl.when(unit < units)
+        def _():
+            h = lax.rem(unit, heads)
+
+            @pl.when(has_behind)
+            def _():
+                forward_copy(unit, mate).wait_recv()
+                summed = weighted(query_far[unit], keys[far_version, h], values[far_version, h])
+                far_out[unit] = summed[:, 0:head].astype(bf16)
+                far_total_out[unit] = total_rows(summed)
+                for copy in far_copies(unit, behind):
+                    copy.start()
+
+            mate_sum[unit] = weighted(
+                query_mate[unit], keys[mate_version, h], values[mate_version, h]
             )
-            query_copy(i).wait_recv()
-
-            @pl.when(has_ahead)
-            def _():
-                forward_copy(i, ahead).start()
-
-            mate_sum[i] = weighted(query_mate[i], keys[mate_version, h], values[mate_version, h])
-
-        @pl.when(jnp.logical_and(has_behind, jnp.logical_and(i >= 1, i < units + 1)))
-        def _():
-            unit = i - 1
-            h = lax.rem(unit, heads)
-            forward_copy(unit, mate).wait_recv()
-            summed = weighted(query_far[unit], keys[far_version, h], values[far_version, h])
-            far_out[unit] = summed[:, 0:head].astype(bf16)
-            far_total_out[unit] = total_rows(summed)
-            for copy in far_copies(unit, behind):
-                copy.start()
-
-        @pl.when(i >= heads + 3)
-        def _():
-            send_back(i - 3)
-
-    @pl.loop(0, heads)
+            own_sum[unit] = weighted(query[unit], keys[0, h], values[0, h]) + weighted(
+                query[unit], text_keys[h], text_values[h]
+            )
+
+        @pl.when(jnp.logical_and(i >= units - ahead_backs, i < units))
+        def _():
+            send_back(i - units + ahead_backs)
+
+        @pl.when(i >= heads + 2 * early)
+        def _():
+            send_back(i - 2 * early)
+
+    @pl.loop(ahead_backs, heads)
     def _(i):
         send_back(i)
 
@@ -295,7 +335,7 @@
             for copy in back_copies(unit):
                 copy.wait_recv()
             total = jnp.transpose(
-                jnp.broadcast_to(back_total_in[unit, 0:1, :], (head, rows))
+                jnp.broadcast_to(back_total_in[unit], (head, rows))
             )
             mine = own_sum[unit]
             attended[half, :, pl.ds(pl.multiple_of(h * head, head), head)] = (
@@ -337,7 +377,6 @@
             tokens_ref[:, here].astype(f32) + modulation_ref[2:3, here] * mixed
         ).astype(bf16)
 
-    fresh_store.wait()
     normed_copy.wait_send()
     mixed_copy.wait_send()
 
@@ -380,24 +419,27 @@
     vmem = pl.BlockSpec(memory_space=pltpu.VMEM)
     hbm = pl.BlockSpec(memory_space=pl.ANY)
     unit_rows = pltpu.VMEM((units, rows, head), bf16)
-    unit_totals = pltpu.VMEM((units, 8, rows), f32)
+    unit_totals = pltpu.VMEM((units, 1, rows), f32)
     unit_sums = pltpu.VMEM((units, rows, 2 * head), f32)
     unit_sems = pltpu.SemaphoreType.DMA((2, units))
     return pl.pallas_call(
         kernel,
         out_shape=(
-            jax.ShapeDtypeStruct(video_tokens.shape, bf16),
-            jax.ShapeDtypeStruct(stale_cache.shape, bf16),
+            pltpu.VMEM(video_tokens.shape, bf16),
+            pltpu.VMEM(stale_cache.shape, bf16),
         ),
-        in_specs=[smem, smem, vmem, vmem, vmem, vmem, hbm, hbm, hbm, hbm],
-        out_specs=(vmem, hbm),
+        in_specs=[smem, smem] + [hbm] * 8,
+        out_specs=(vmem, vmem),
         scratch_shapes=[
+            pltpu.VMEM(video_tokens.shape, bf16),
+            pltpu.VMEM(modulation.shape, f32),
+            pltpu.VMEM(norm_gains.shape, f32),
+            pltpu.VMEM(video_keep.shape, jnp.int32),
             pltpu.VMEM(project_weight.shape, bf16),
             pltpu.VMEM(output_weight.shape, bf16),
             pltpu.VMEM(text_cache.shape, bf16),
             pltpu.VMEM(stale_cache.shape, bf16),
             pltpu.VMEM((2, rows, model), bf16),
-            pltpu.VMEM(stale_cache.shape, bf16),
             unit_rows,
             unit_rows,
             unit_rows,
@@ -418,8 +460,7 @@
             pltpu.VMEM((2, rows, width), bf16),
             pltpu.VMEM((rows, model), bf16),
             pltpu.VMEM((rows, model), bf16),
-            pltpu.SemaphoreType.DMA((6,)),
-            pltpu.SemaphoreType.DMA,
+            pltpu.SemaphoreType.DMA((10,)),
             pltpu.SemaphoreType.DMA((2,)),
             unit_sems,
             unit_sems,
@@ -438,7 +479,7 @@
         video_tokens,
         modulation,
         norm_gains,
-        video_keep.reshape(-1, patch),
+        video_keep,
         project_weight,
         output_weight,
         text_cache,

time: 64.9 us -> 49.9 us (0.77)
  Pallas kernels: 58.7 us -> 46.4 us
  local copies, waits for them, and re-layouts: 4.65 us -> 2.02 us
    pallas_call x1, Pallas kernels: 58.7 us -> 46.4 us  [on_device(): pl.pallas_call(kernel, out_shape=(pltpu.VMEM(video_tokens.shape, bf16), p...]
    reshape x1 -> x0, local copies, waits for them, and re-layouts: 1.33 us -> none  [on_device(): video_keep.reshape(-1, patch)]
    unnamed x4 -> x2, local copies, waits for them, and re-layouts: 3.33 us -> 2.02 us
where the time goes in v2:
time: 49.9 us; the launch traced here: 49.7 us
  Pallas kernels  46.4 us (93%)
  local copies, waits for them, and re-layouts  2.02 us (4%)
  between operations  1.29 us (3%)
    pallas_call x1, Pallas kernels, on_device(): pl.pallas_call(kernel, out_shape=(pltpu.VMEM(video_tokens.shape, bf16), p...  46.4 us
    unnamed x2, local copies, waits for them, and re-layouts  2.02 us

profile of v2, /device:TPU:0, one launch (start us, length us, event | category | flops | bytes accessed | tf_op | source)
XLA Modules:
  0.0 49.7 jit_solution(9104276368744951492)
XLA Ops:
  1.3 46.4 %shard_map.113 = (bf16[256,1536]{1,0:T(8,128)(2,1)S(1)}, bf16[2,512,768]{2,1,0:T(8,128)(2,1)S(1)}) custom-call(s32[8]{0:T(128)} %order_ref.1, s32[1]{0:T(128)S(6)} %copy.16.count_ref, bf16[256,1536]{1,0:T(8,128)(2,1)} %tokens_hbm.1, f32[3,1536]{1,0:T(4,128)} %modulation_hbm.1, f32[3,128]{1,0:T(4,128)} %gains_hbm.1, s32[4096]{0:T(1024)} %keep_hbm.1, ...), custom_call_target="tpu_custom_call" | custom-call | tf_op jit(solution)/shard_map/pallas_call | solution.py:425
  47.7 0.9 %copy.14 = bf16[256,1536]{1,0:T(8,128)(2,1)} copy(bf16[256,1536]{1,0:T(8,128)(2,1)S(1)} %get-tuple-element.2) | data formatting | bytes 1572864
  48.6 1.1 %copy.15 = bf16[2,512,768]{2,1,0:T(8,128)(2,1)} copy(bf16[2,512,768]{2,1,0:T(8,128)(2,1)S(1)} %get-tuple-element.3) | data formatting | bytes 3145728

commit v3 on v2

--- a/solution.py
+++ b/solution.py
@@ -62,6 +62,7 @@
     attended,
     mixed_out,
     mixed_in,
+    partial,
     load_sem,
     normed_sem,
     query_sem,
@@ -328,8 +329,8 @@
     def _(i):
         send_back(i)
 
-    def gather_back(half):
-        @pl.loop(0, heads)
+    def gather_range(half, first, last):
+        @pl.loop(first, last)
         def _(h):
             unit = half * heads + h
             for copy in back_copies(unit):
@@ -354,7 +355,7 @@
     full = output_weight.shape[1]
     wide = 512 if full % 512 == 0 else full
 
-    gather_back(1)
+    gather_range(1, 0, heads)
     loads[5].wait()
 
     @pl.loop(0, full // wide)
@@ -365,14 +366,35 @@
         ).astype(bf16)
 
     mixed_copy.start()
-    gather_back(0)
-    mixed_copy.wait_recv()
+    split = heads - min(2, heads - 1)
+    gather_range(0, 0, split)
 
     @pl.loop(0, full // wide)
     def _(c):
         here = pl.ds(pl.multiple_of(c * wide, wide), wide)
-        mixed = jnp.dot(attended[0], output_weight[:, here], preferred_element_type=f32)
-        mixed = mixed + mixed_in[:, here].astype(f32)
+        partial[:, here] = jnp.dot(
+            attended[0, :, 0 : split * head],
+            output_weight[0 : split * head, here],
+            preferred_element_type=f32,
+        )
+
+    mixed_copy.wait_recv()
+
+    @pl.loop(0, full // wide)
+    def _(c):
+        here = pl.ds(pl.multiple_of(c * wide, wide), wide)
+        partial[:, here] = partial[:, here] + mixed_in[:, here].astype(f32)
+
+    gather_range(0, split, heads)
+
+    @pl.loop(0, full // wide)
+    def _(c):
+        here = pl.ds(pl.multiple_of(c * wide, wide), wide)
+        mixed = partial[:, here] + jnp.dot(
+            attended[0, :, split * head :],
+            output_weight[split * head :, here],
+            preferred_element_type=f32,
+        )
         updated_ref[:, here] = (
             tokens_ref[:, here].astype(f32) + modulation_ref[2:3, here] * mixed
         ).astype(bf16)
@@ -460,6 +482,7 @@
             pltpu.VMEM((2, rows, width), bf16),
             pltpu.VMEM((rows, model), bf16),
             pltpu.VMEM((rows, model), bf16),
+            pltpu.VMEM((rows, model), f32),
             pltpu.SemaphoreType.DMA((10,)),
             pltpu.SemaphoreType.DMA((2,)),
             unit_sems,

time: 49.9 us -> 49.4 us (0.990)
  no operation moved by 1% of the time
where the time goes in v3:
time: 49.4 us; the launch traced here: 49.3 us
  Pallas kernels  46 us (93%)
  local copies, waits for them, and re-layouts  2.02 us (4%)
  between operations  1.29 us (3%)
    pallas_call x1, Pallas kernels, on_device(): pl.pallas_call(kernel, out_shape=(pltpu.VMEM(video_tokens.shape, bf16), p...  46 us
    unnamed x2, local copies, waits for them, and re-layouts  2.02 us

profile of v3, /device:TPU:0, one launch (start us, length us, event | category | flops | bytes accessed | tf_op | source)
XLA Modules:
  0.0 49.3 jit_solution(9242026199352450201)
XLA Ops:
  1.3 46.0 %shard_map.113 = (bf16[256,1536]{1,0:T(8,128)(2,1)S(1)}, bf16[2,512,768]{2,1,0:T(8,128)(2,1)S(1)}) custom-call(s32[8]{0:T(128)} %order_ref.1, s32[1]{0:T(128)S(6)} %copy.16.count_ref, bf16[256,1536]{1,0:T(8,128)(2,1)} %tokens_hbm.1, f32[3,1536]{1,0:T(4,128)} %modulation_hbm.1, f32[3,128]{1,0:T(4,128)} %gains_hbm.1, s32[4096]{0:T(1024)} %keep_hbm.1, ...), custom_call_target="tpu_custom_call" | custom-call | tf_op jit(solution)/shard_map/pallas_call | solution.py:447
  47.2 0.9 %copy.14 = bf16[256,1536]{1,0:T(8,128)(2,1)} copy(bf16[256,1536]{1,0:T(8,128)(2,1)S(1)} %get-tuple-element.2) | data formatting | bytes 1572864
  48.1 1.1 %copy.15 = bf16[2,512,768]{2,1,0:T(8,128)(2,1)} copy(bf16[2,512,768]{2,1,0:T(8,128)(2,1)S(1)} %get-tuple-element.3) | data formatting | bytes 3145728
